TPU v7x, 32 devices: a whole 2x2x4 slice. The times are simulated.
32 devices in a mesh: groups: 2 (over x), hst: 8 (over z, y), head: 2 (over core).
Axes of the slice: x: 2, y: 2, z: 4, core: 2. Of those that a mesh axis runs over, the one named last changes fastest.
Arguments:
- ctx_query: bfloat16 [3072, 64, 128], P(('groups', 'hst'), 'head'), parts along dimension 0, may hold values from -8 to 8
- ctx_key: bfloat16 [3072, 64, 128], P(('groups', 'hst'), 'head'), parts along dimension 0, may hold values from -8 to 8
- ctx_value: bfloat16 [3072, 64, 128], P(('groups', 'hst'), 'head'), parts along dimension 0, may hold values from -6 to 6
- valid: int32 [16], P(('groups', 'hst')), parts along dimension 0, may hold values from 128 to 192
- tail_query: bfloat16 [128, 64, 128], P(('groups', 'hst'), 'head'), parts along dimension 0, may hold values from -8 to 8
- tail_position: int32 [128], P(('groups', 'hst')), parts along dimension 0, may hold values from 1 to 1536
Outputs:
- ctx_out: bfloat16 [3072, 64, 128], P(('groups', 'hst'), 'head'), parts along dimension 0
- tail_out: bfloat16 [128, 64, 128], P(('groups', 'hst'), 'head'), parts along dimension 0
There are 2 independent parts, one for each index of `groups`. A program takes and returns all parts, laid end to end along the dimension named above; each array names one. Nothing has to cross between parts.
All inputs are finite; a program needn't handle non-finite values.
Results may differ from a plain program's by a relative error of at most 0.0043.
Values may be sent and summed in bfloat16 or wider, within the bound.
No kernel may reach another device: no remote copies, remote signals or barrier semaphores. Data moves between devices by JAX's collectives and lax.ppermute only.
A program may use at most 128 MiB of HBM per device.

v0:
```python
import math
import jax
import jax.numpy as jnp
from jax import lax
from jax.sharding import PartitionSpec as P

ANCHOR = 128


def broadcast(array, axis, root):
    mine = lax.axis_index(axis) == root
    return lax.psum(jnp.where(mine, array, jnp.zeros_like(array)), axis)


def masked_softmax(scores, mask):
    scores = jnp.where(mask, scores, jnp.float32(-1e30))
    peak = jnp.max(scores, axis=-1)
    weights = jnp.where(mask, jnp.exp(scores - peak[..., None]), jnp.float32(0.0))
    return (peak, weights, jnp.sum(weights, axis=-1))


def local(ctx_query, ctx_key, ctx_value, valid, tail_query, tail_position):
    block, heads, width = ctx_query.shape
    scale = 1.0 / math.sqrt(width)
    host = lax.axis_index("hst")
    anchor_key, anchor_value = (
        broadcast(ctx_key[:ANCHOR], "hst", 0),
        broadcast(ctx_value[:ANCHOR], "hst", 0),
    )
    own_count = valid[0]
    keys = jnp.concatenate([anchor_key, ctx_key], 0)
    values = jnp.concatenate([anchor_value, ctx_value], 0)
    rows = jnp.arange(block)[:, None]
    cols = jnp.arange(block)[None, :]
    own_mask = (cols <= rows) & (cols < own_count)
    anchor_mask = jnp.broadcast_to(host != 0, (block, ANCHOR))
    mask = jnp.concatenate([anchor_mask, own_mask], 1)
    scores = jnp.einsum("qhd,khd->hqk", ctx_query, keys, preferred_element_type=jnp.float32) * scale
    peak, weights, total = masked_softmax(scores, mask[None])
    summed = jnp.einsum(
        "hqk,khd->qhd", weights.astype(jnp.bfloat16), values, preferred_element_type=jnp.float32
    )
    ctx_out = (summed / jnp.transpose(total)[:, :, None]).astype(jnp.bfloat16)
    far_key, far_value, far_query = (
        lax.all_to_all(ctx_key, "hst", split_axis=1, concat_axis=0, tiled=True),
        lax.all_to_all(ctx_value, "hst", split_axis=1, concat_axis=0, tiled=True),
        lax.all_to_all(tail_query, "hst", split_axis=1, concat_axis=0, tiled=True),
    )
    counts, positions = (
        lax.all_gather(valid, "hst", axis=0, tiled=True),
        lax.all_gather(tail_position, "hst", axis=0, tiled=True),
    )
    starts = jnp.cumsum(counts) - counts
    slots = jnp.arange(block)
    key_places = (starts[:, None] + slots[None, :]).reshape(-1)
    live = (slots[None, :] < counts[:, None]).reshape(-1)
    row_mask = live[None, :] & (key_places[None, :] < positions[:, None])
    tail_scores = (
        jnp.einsum("rhd,khd->hrk", far_query, far_key, preferred_element_type=jnp.float32) * scale
    )
    tail_peak, tail_weights, tail_total = masked_softmax(tail_scores, row_mask[None])
    tail_summed = jnp.einsum(
        "hrk,khd->rhd", tail_weights, far_value.astype(jnp.float32), precision=lax.Precision.HIGHEST
    )
    result = (tail_summed / jnp.transpose(tail_total)[:, :, None]).astype(jnp.bfloat16)
    tail_out = lax.all_to_all(result, "hst", split_axis=0, concat_axis=1, tiled=True)
    return (ctx_out, tail_out)


def solution(mesh):
    in_specs = (
        P(("groups", "hst"), "head", None),
        P(("groups", "hst"), "head", None),
        P(("groups", "hst"), "head", None),
        P(("groups", "hst")),
        P(("groups", "hst"), "head", None),
        P(("groups", "hst")),
    )
    out_specs = (P(("groups", "hst"), "head", None), P(("groups", "hst"), "head", None))
    return jax.shard_map(local, mesh=mesh, in_specs=in_specs, out_specs=out_specs, check_vma=False)
```

profile of v0, /device:TPU:0, one launch (start us, length us, event | category | flops | bytes accessed | tf_op | source)
XLA Modules:
  0.0 242.4 jit_solution(3953943348192276413)
XLA Ops:
  7.2 3.3 %copy.20 = bf16[192,32,128]{2,0,1:T(8,128)(2,1)} copy(bf16[192,32,128]{2,1,0:T(8,128)(2,1)} %param.7) | data formatting | bytes 3145728 | tf_op args[1]
  10.5 7.3 %all-to-all-start.1 = ((bf16[192,32,128]{2,0,1:T(8,128)(2,1)}), bf16[192,32,128]{2,0,1:T(8,128)(2,1)S(1)}, u32[]{:S(2)}, u32[]{:S(2)}) async-start(bf16[192,32,128]{2,0,1:T(8,128)(2,1)} %copy.20), calls=%async_computation.1 | async-start | bytes 3145728 | tf_op jit(solution)/shard_map/all_to_all | solution.py:45
  17.8 3.2 %copy.18 = bf16[192,32,128]{2,0,1:T(8,128)(2,1)} copy(bf16[192,32,128]{2,1,0:T(8,128)(2,1)} %param.8) | data formatting | bytes 3145728 | tf_op args[2]
  20.9 2.3 slice_select_fusion.1
  23.2 31.6 %all-to-all-done.1 = bf16[192,32,128]{2,0,1:T(8,128)(2,1)S(1)} async-done(((bf16[192,32,128]{2,0,1:T(8,128)(2,1)}), bf16[192,32,128]{2,0,1:T(8,128)(2,1)S(1)}, u32[]{:S(2)}, u32[]{:S(2)}) %all-to-all-start.1) | async-done | bytes 1572896 | tf_op jit(solution)/shard_map/all_to_all | solution.py:45
  54.8 4.3 %all-to-all-start.2 = ((bf16[192,32,128]{2,0,1:T(8,128)(2,1)}), bf16[192,32,128]{2,0,1:T(8,128)(2,1)}, u32[]{:S(2)}, u32[]{:S(2)}) async-start(bf16[192,32,128]{2,0,1:T(8,128)(2,1)} %copy.18), calls=%async_computation.2 | async-start | bytes 3145728 | tf_op jit(solution)/shard_map/all_to_all | solution.py:46
  59.1 2.3 slice_select_fusion
  63.6 0.8 dynamic-update-slice
  64.4 54.1 %all-reduce.3 = (s32[8]{0:T(128)S(1)}, s32[64]{0:T(128)S(1)}) all-reduce(s32[8]{0:T(128)S(1)} %dynamic-update-slice, s32[64]{0:T(128)S(1)} %dynamic-update-slice.1), channel_id=1, replica_groups=mesh['groups'=2,'hst'=8,'head'=2] {'hst'}, use_global_device_ids=true, to_apply=%add.1 | all-reduce | flops 72 | bytes 576
  119.0 0.7 copy.23
  119.9 68.3 %all-reduce.7.cloned.1.call-done = (bf16[128,32,128]{2,0,1:T(8,128)(2,1)}, bf16[128,32,128]{2,0,1:T(8,128)(2,1)}) async-done(((bf16[128,32,128]{2,0,1:T(8,128)(2,1)}, bf16[128,32,128]{2,0,1:T(8,128)(2,1)}), (bf16[128,32,128]{2,0,1:T(8,128)(2,1)}, bf16[128,32,128]{2,0,1:T(8,128)(2,1)})) %all-reduce.7.cloned.1.call-update) | async-done | bytes 2097168 | tf_op jit(solution)/shard_map/psum | solution.py:12
  188.2 6.8 %fusion.9 = f32[32,320,192]{1,2,0:T(8,128)} fusion(bf16[192,32,128]{2,0,1:T(8,128)(2,1)} %copy.20, bf16[128,32,128]{2,0,1:T(8,128)(2,1)} %get-tuple-element.8, bf16[192,32,128]{2,1,0:T(8,128)(2,1)S(1)} %copy-done), kind=kOutput, calls=%fused_computation.13 | convolution fusion | flops 508559360 | bytes 12058624 | tf_op jit(solution)/shard_map/qhd,khd->hqk/dot_general | solution.py:38
  195.0 3.9 %all-to-all-start = ((bf16[8,32,128]{2,0,1:T(8,128)(2,1)}), bf16[8,32,128]{2,0,1:T(8,128)(2,1)S(1)}, u32[]{:S(2)}, u32[]{:S(2)}) async-start(bf16[8,32,128]{2,0,1:T(8,128)(2,1)} %copy.23), calls=%async_computation | async-start | bytes 131072 | tf_op jit(solution)/shard_map/all_to_all | solution.py:47
  198.9 14.9 %fusion.37 = (f32[32,192]{1,0:T(8,128)S(1)}, bf16[32,192,320]{2,1,0:T(8,128)(2,1)}) fusion(f32[32,320,192]{1,2,0:T(8,128)} %fusion.9, pred[192,320]{1,0:T(8,128)(4,1)S(1)} %concatenate.10), kind=kOutput, calls=%fused_computation.46 | output fusion | flops 15728959 | bytes 11882496 | tf_op jit(solution)/shard_map/sub | solution.py:18
  213.8 1.3 copy.26
  215.1 2.8 %copy.28 = bf16[192,8,4,128]{3,0,1,2:T(8,128)(2,1)} copy(bf16[192,8,4,128]{3,0,2,1:T(8,128)(2,1)} %bitcast.14) | data formatting | bytes 3145728 | tf_op jit(solution)/shard_map/all_to_all | solution.py:46
  217.9 0.8 fusion.38
  219.1 1.0 copy-done.2
  220.0 1.3 fusion.21
  221.4 0.7 copy.29
  222.0 6.0 %all-to-all-start.3 = ((bf16[64,4,128]{2,1,0:T(4,128)(2,1)}), bf16[64,4,128]{2,1,0:T(4,128)(2,1)S(1)}, u32[]{:S(2)}, u32[]{:S(2)}) async-start(bf16[64,4,128]{2,1,0:T(4,128)(2,1)} %copy.29), calls=%async_computation.3 | async-start | bytes 131072 | tf_op jit(solution)/shard_map/all_to_all | solution.py:66
  228.0 4.2 %fusion.7 = bf16[192,32,128]{2,0,1:T(8,128)(2,1)S(1)} fusion(f32[192,32]{0,1:T(8,128)S(1)} %bitcast.61, bf16[192,32,128]{2,0,1:T(8,128)(2,1)} %copy.18, bf16[128,32,128]{2,0,1:T(8,128)(2,1)S(1)} %copy-done.4, bf16[32,192,320]{2,1,0:T(8,128)(2,1)} %get-tuple-element.11), kind=kOutput, calls=%fused_computation.10 | convolution fusion | flops 510132224 | bytes 8151040 | tf_op jit(solution)/shard_map/hqk,khd->qhd/dot_general | solution.py:40
  232.3 2.2 copy.31
  234.9 0.7 copy.30
  (33 shorter events, 2.6 us)
Async XLA Ops:
  7.2 181.0 %copy-start = (bf16[192,32,128]{2,1,0:T(8,128)(2,1)S(1)}, bf16[192,32,128]{2,1,0:T(8,128)(2,1)}, u32[]{:S(2)}) copy-start(bf16[192,32,128]{2,1,0:T(8,128)(2,1)} %param.6) | copy-start | bytes 4718596
  10.5 44.3 %all-to-all-start.1 = ((bf16[192,32,128]{2,0,1:T(8,128)(2,1)}), bf16[192,32,128]{2,0,1:T(8,128)(2,1)S(1)}, u32[]{:S(2)}, u32[]{:S(2)}) async-start(bf16[192,32,128]{2,0,1:T(8,128)(2,1)} %copy.20), calls=%async_computation.1 | async-start | bytes 3145728 | tf_op jit(solution)/shard_map/all_to_all | solution.py:45
  54.8 140.2 %all-to-all-start.2 = ((bf16[192,32,128]{2,0,1:T(8,128)(2,1)}), bf16[192,32,128]{2,0,1:T(8,128)(2,1)}, u32[]{:S(2)}, u32[]{:S(2)}) async-start(bf16[192,32,128]{2,0,1:T(8,128)(2,1)} %copy.18), calls=%async_computation.2 | async-start | bytes 3145728 | tf_op jit(solution)/shard_map/all_to_all | solution.py:46
  59.1 129.1 %all-reduce.7.cloned.1.call-start = ((), (), s32[]{:S(2)}) async-start(), calls=%async_computation.4 | async-start | bytes 4194304 | tf_op jit(solution)/shard_map/psum | solution.py:12
  61.4 0.7 copy-start.6
  61.4 2.0 copy-start.5
  61.4 57.6 %copy-start.3 = (bf16[8,32,128]{2,1,0:T(8,128)(2,1)S(1)}, bf16[8,32,128]{2,1,0:T(8,128)(2,1)}, u32[]{:S(2)}) copy-start(bf16[8,32,128]{2,1,0:T(8,128)(2,1)} %param.10) | copy-start | bytes 196612
  195.0 22.9 %all-to-all-start = ((bf16[8,32,128]{2,0,1:T(8,128)(2,1)}), bf16[8,32,128]{2,0,1:T(8,128)(2,1)S(1)}, u32[]{:S(2)}, u32[]{:S(2)}) async-start(bf16[8,32,128]{2,0,1:T(8,128)(2,1)} %copy.23), calls=%async_computation | async-start | bytes 131072 | tf_op jit(solution)/shard_map/all_to_all | solution.py:47
  215.1 2.8 %copy-start.1 = (bf16[192,8,4,128]{3,0,1,2:T(8,128)(2,1)S(1)}, bf16[192,8,4,128]{3,0,1,2:T(8,128)(2,1)}, u32[]{:S(2)}) copy-start(bf16[192,8,4,128]{3,0,1,2:T(8,128)(2,1)} %copy.26) | copy-start | bytes 4718596
  218.6 1.4 copy-start.2
  220.0 8.0 %copy-start.4 = (bf16[128,32,128]{2,0,1:T(8,128)(2,1)S(1)}, bf16[128,32,128]{2,0,1:T(8,128)(2,1)}, u32[]{:S(2)}) copy-start(bf16[128,32,128]{2,0,1:T(8,128)(2,1)} %get-tuple-element.9) | copy-start | bytes 3145732
  222.0 12.9 %all-to-all-start.3 = ((bf16[64,4,128]{2,1,0:T(4,128)(2,1)}), bf16[64,4,128]{2,1,0:T(4,128)(2,1)S(1)}, u32[]{:S(2)}, u32[]{:S(2)}) async-start(bf16[64,4,128]{2,1,0:T(4,128)(2,1)} %copy.29), calls=%async_computation.3 | async-start | bytes 131072 | tf_op jit(solution)/shard_map/all_to_all | solution.py:66
Sparse Core Ops, SparseCore 0:
  63.6 124.5 all-reduce.6
where the time goes:
time: 243 us; the launch traced here: 242 us
  waiting for transfers between devices  100 us (41%)
  blocking collectives  54.1 us (22%)
  starting transfers between devices  21.6 us (9%)
  other arithmetic  20.3 us (8%)
  local copies, waits for them, and re-layouts  17.5 us (7%)
  between operations  15.5 us (6%)
  matrix products  13.1 us (5%)
    psum x1, waiting for transfers between devices, broadcast(): return lax.psum(jnp.where(mine, array, jnp.zeros_like(array)), axis)  68.3 us
    unnamed x1, blocking collectives  54.1 us
    all_to_all x1, waiting for transfers between devices, local(): lax.all_to_all(ctx_key, 'hst', split_axis=1, concat_axis=0, tiled=True)  31.6 us
    sub x1, other arithmetic, masked_softmax(): scores - peak[..., None]  14.9 us
    unnamed x23, local copies, waits for them, and re-layouts  11.9 us
    all_to_all x1, starting transfers between devices, local(): lax.all_to_all(ctx_key, 'hst', split_axis=1, concat_axis=0, tiled=True)  7.31 us
    dot_general x1, matrix products, local(): jnp.einsum('qhd,khd->hqk', ctx_query, keys, preferred_element_type=jnp.fl...  6.84 us
    all_to_all x1, starting transfers between devices, local(): lax.all_to_all(result, 'hst', split_axis=0, concat_axis=1, tiled=True)  6 us
  transfers between devices with their start and end apart: 5, of which 3 were waited for; matrix products, arithmetic and copies ran while one was open for 18% of the time, Pallas kernels for 0%

commit v1 on v0

--- a/solution.py
+++ b/solution.py
@@ -7,9 +7,15 @@
 ANCHOR = 128
 
 
+def gather_and_add(x, axis):
+    blocks = lax.all_gather(x, axis, axis=0, tiled=False)
+    summed = blocks.sum(axis=0)
+    return summed
+
+
 def broadcast(array, axis, root):
     mine = lax.axis_index(axis) == root
-    return lax.psum(jnp.where(mine, array, jnp.zeros_like(array)), axis)
+    return gather_and_add(jnp.where(mine, array, jnp.zeros_like(array)), axis)
 
 
 def masked_softmax(scores, mask):

time: 243 us -> 368 us (1.51)
  waiting for transfers between devices: 100 us -> 197 us
  blocking collectives: 54.1 us -> 76.6 us
  other arithmetic: 20.3 us -> 29.2 us
    all_gather x0 -> x2, waiting for transfers between devices: none -> 120 us  [gather_and_add(): blocks = lax.all_gather(x, axis, axis=0, tiled=False)]
    psum x1 -> x0, waiting for transfers between devices: 68.3 us -> none  [broadcast(): return lax.psum(jnp.where(mine, array, jnp.zeros_like(array)), axis)]
    all_to_all x1, waiting for transfers between devices: 31.6 us -> 67.4 us  [local(): lax.all_to_all(ctx_key, 'hst', split_axis=1, concat_axis=0, tiled=True)]
    unnamed x1, blocking collectives: 54.1 us -> 76.6 us
    reduce_sum x0 -> x2, other arithmetic: none -> 10.5 us  [gather_and_add(): summed = blocks.sum(axis=0)]
    all_to_all x1, waiting for transfers between devices: 0.51 us -> 6.59 us  [local(): lax.all_to_all(result, 'hst', split_axis=0, concat_axis=1, tiled=True)]
    unnamed x23 -> x25, local copies, waits for them, and re-layouts: 11.9 us -> 11.2 us
  transfers between devices with their start and end apart: 5 -> 6, of which waited for: 3 -> 5; matrix products, arithmetic and copies ran while one was open for 18% -> 7% of each run, Pallas kernels for 0% -> 0%
where the time goes in v1:
time: 368 us; the launch traced here: 367 us
  waiting for transfers between devices  197 us (54%)
  blocking collectives  76.6 us (21%)
  other arithmetic  29.2 us (8%)
  local copies, waits for them, and re-layouts  18.7 us (5%)
  starting transfers between devices  18.6 us (5%)
  between operations  15.5 us (4%)
  matrix products  11.3 us (3%)
    all_gather x2, waiting for transfers between devices, gather_and_add(): blocks = lax.all_gather(x, axis, axis=0, tiled=False)  120 us
    unnamed x1, blocking collectives  76.6 us
    all_to_all x1, waiting for transfers between devices, local(): lax.all_to_all(ctx_key, 'hst', split_axis=1, concat_axis=0, tiled=True)  67.4 us
    sub x1, other arithmetic, masked_softmax(): scores - peak[..., None]  13 us
    unnamed x25, local copies, waits for them, and re-layouts  11.2 us
    reduce_sum x2, other arithmetic, gather_and_add(): summed = blocks.sum(axis=0)  10.5 us
  transfers between devices with their start and end apart: 6, of which 5 were waited for; matrix products, arithmetic and copies ran while one was open for 7% of the time, Pallas kernels for 0%

profile of v1, /device:TPU:0, one launch (start us, length us, event | category | flops | bytes accessed | tf_op | source)
XLA Modules:
  0.0 367.0 jit_solution(4760555891693292444)
XLA Ops:
  7.2 2.4 slice_select_fusion
  9.7 2.4 slice_select_fusion.1
  12.1 1.8 copy.19
  13.9 7.3 %all-to-all-start.1 = ((bf16[192,32,128]{2,0,1:T(8,128)(2,1)}), bf16[192,32,128]{2,0,1:T(8,128)(2,1)S(1)}, u32[]{:S(2)}, u32[]{:S(2)}) async-start(bf16[192,32,128]{2,0,1:T(8,128)(2,1)} %copy.19), calls=%async_computation.1 | async-start | bytes 3145728 | tf_op jit(solution)/shard_map/all_to_all | solution.py:51
  21.2 3.3 copy.17
  24.5 67.4 %all-to-all-done.1 = bf16[192,32,128]{2,0,1:T(8,128)(2,1)S(1)} async-done(((bf16[192,32,128]{2,0,1:T(8,128)(2,1)}), bf16[192,32,128]{2,0,1:T(8,128)(2,1)S(1)}, u32[]{:S(2)}, u32[]{:S(2)}) %all-to-all-start.1) | async-done | bytes 1572896 | tf_op jit(solution)/shard_map/all_to_all | solution.py:51
  91.9 4.3 %all-to-all-start.2 = ((bf16[192,32,128]{2,0,1:T(8,128)(2,1)}), bf16[192,32,128]{2,0,1:T(8,128)(2,1)}, u32[]{:S(2)}, u32[]{:S(2)}) async-start(bf16[192,32,128]{2,0,1:T(8,128)(2,1)} %copy.17), calls=%async_computation.2 | async-start | bytes 3145728 | tf_op jit(solution)/shard_map/all_to_all | solution.py:52
  99.1 76.6 %all-reduce.3 = (s32[8]{0:T(128)S(1)}, s32[64]{0:T(128)S(1)}) all-reduce(s32[8]{0:T(128)S(1)} %dynamic-update-slice, s32[64]{0:T(128)S(1)} %dynamic-update-slice.1), channel_id=1, replica_groups=mesh['groups'=2,'hst'=8,'head'=2] {'hst'}, use_global_device_ids=true, to_apply=%add.1 | all-reduce | flops 72 | bytes 576
  176.8 3.4 all-to-all-start
  180.4 1.3 copy.24
  181.7 2.8 copy.26
  184.5 3.5 all-to-all-done
  189.2 1.0 copy-done.4
  190.2 1.3 fusion.21
  192.2 3.5 all-to-all-start.3
  195.8 6.6 %all-to-all-done.3 = bf16[64,4,128]{2,1,0:T(4,128)(2,1)S(1)} async-done(((bf16[64,4,128]{2,1,0:T(4,128)(2,1)}), bf16[64,4,128]{2,1,0:T(4,128)(2,1)S(1)}, u32[]{:S(2)}, u32[]{:S(2)}) %all-to-all-start.3) | async-done | bytes 65568 | tf_op jit(solution)/shard_map/all_to_all | solution.py:72
  203.6 5.2 %reduce_sum.43 = bf16[128,32,128]{2,1,0:T(8,128)(2,1)S(1)} reduce(bf16[8,128,32,128]{3,2,1,0:T(8,128)(2,1)} %bitcast.55, bf16[]{:T(256)} %constant.7.clone.1), dimensions={0}, to_apply=%region_1.2 | reduce | flops 3670016 | bytes 9437186 | tf_op jit(solution)/shard_map/reduce_sum | solution.py:12
  208.9 1.4 copy.18
  210.2 119.0 %all-gather.5.cloned.1.call-done = bf16[1024,32,128]{2,1,0:T(8,128)(2,1)} async-done(((bf16[128,32,128]{2,1,0:T(8,128)(2,1)}), bf16[1024,32,128]{2,1,0:T(8,128)(2,1)}) %all-gather.5.cloned.1.call-update) | async-done | bytes 8388624 | tf_op jit(solution)/shard_map/all_gather | solution.py:11
  329.2 5.2 %reduce_sum.42 = bf16[128,32,128]{2,1,0:T(8,128)(2,1)S(1)} reduce(bf16[8,128,32,128]{3,2,1,0:T(8,128)(2,1)} %bitcast.56, bf16[]{:T(256)} %constant.7.clone.1), dimensions={0}, to_apply=%region_0.1 | reduce | flops 3670016 | bytes 9437186 | tf_op jit(solution)/shard_map/reduce_sum | solution.py:12
  335.7 6.6 %fusion.9 = f32[32,320,192]{1,2,0:T(8,128)} fusion(bf16[192,32,128]{2,0,1:T(8,128)(2,1)} %copy.19, bf16[128,32,128]{2,0,1:T(8,128)(2,1)S(1)} %copy-done.3, bf16[192,32,128]{2,1,0:T(8,128)(2,1)S(1)} %copy-done), kind=kOutput, calls=%fused_computation.13 | convolution fusion | flops 508559360 | bytes 12058624 | tf_op jit(solution)/shard_map/qhd,khd->hqk/dot_general | solution.py:44
  342.3 13.0 %fusion.37 = (f32[32,192]{1,0:T(8,128)S(1)}, bf16[32,192,320]{2,1,0:T(8,128)(2,1)S(1)}) fusion(f32[32,320,192]{1,2,0:T(8,128)} %fusion.9, pred[192,320]{1,0:T(8,128)(4,1)S(1)} %concatenate.10), kind=kOutput, calls=%fused_computation.46 | output fusion | flops 15728959 | bytes 11882496 | tf_op jit(solution)/shard_map/sub | solution.py:24
  355.3 2.7 fusion.7
  358.0 2.2 copy.29
  (42 shorter events, 7.4 us)
Async XLA Ops:
  7.2 327.8 %copy-start = (bf16[192,32,128]{2,1,0:T(8,128)(2,1)S(1)}, bf16[192,32,128]{2,1,0:T(8,128)(2,1)}, u32[]{:S(2)}) copy-start(bf16[192,32,128]{2,1,0:T(8,128)(2,1)} %param.6) | copy-start | bytes 4718596
  7.2 196.4 %all-gather.7.cloned.1.call-start = ((), (), s32[]{:S(2)}) async-start(), calls=%async_computation.5 | async-start | bytes 9437184 | tf_op jit(solution)/shard_map/all_gather | solution.py:11
  9.6 2.5 copy-start.2
  9.7 319.6 %all-gather.5.cloned.1.call-start = ((), (), s32[]{:S(2)}) async-start(), calls=%async_computation.4 | async-start | bytes 9437184 | tf_op jit(solution)/shard_map/all_gather | solution.py:11
  13.9 78.0 %all-to-all-start.1 = ((bf16[192,32,128]{2,0,1:T(8,128)(2,1)}), bf16[192,32,128]{2,0,1:T(8,128)(2,1)S(1)}, u32[]{:S(2)}, u32[]{:S(2)}) async-start(bf16[192,32,128]{2,0,1:T(8,128)(2,1)} %copy.19), calls=%async_computation.1 | async-start | bytes 3145728 | tf_op jit(solution)/shard_map/all_to_all | solution.py:51
  24.5 72.4 %copy-start.7 = (u32[32]{0:T(128)S(1)}, u32[32]{0:T(128)}, u32[]{:S(2)}) copy-start(u32[32]{0:T(128)} %constant.31) | copy-start | bytes 388
  24.5 74.4 %copy-start.6 = (s32[8]{0:T(128)S(1)}, s32[8]{0:T(128)}, u32[]{:S(2)}) copy-start(s32[8]{0:T(128)} %param.11) | copy-start | bytes 100
  24.5 151.7 %copy-start.5 = (bf16[8,32,128]{2,1,0:T(8,128)(2,1)S(1)}, bf16[8,32,128]{2,1,0:T(8,128)(2,1)}, u32[]{:S(2)}) copy-start(bf16[8,32,128]{2,1,0:T(8,128)(2,1)} %param.10) | copy-start | bytes 196612
  91.9 85.0 %all-to-all-start.2 = ((bf16[192,32,128]{2,0,1:T(8,128)(2,1)}), bf16[192,32,128]{2,0,1:T(8,128)(2,1)}, u32[]{:S(2)}, u32[]{:S(2)}) async-start(bf16[192,32,128]{2,0,1:T(8,128)(2,1)} %copy.17), calls=%async_computation.2 | async-start | bytes 3145728 | tf_op jit(solution)/shard_map/all_to_all | solution.py:52
  176.8 11.1 %all-to-all-start = ((bf16[8,32,128]{2,0,1:T(8,128)(2,1)}), bf16[8,32,128]{2,0,1:T(8,128)(2,1)S(1)}, u32[]{:S(2)}, u32[]{:S(2)}) async-start(bf16[8,32,128]{2,0,1:T(8,128)(2,1)} %copy.21), calls=%async_computation | async-start | bytes 131072 | tf_op jit(solution)/shard_map/all_to_all | solution.py:53
  181.7 6.3 %copy-start.1 = (bf16[192,8,4,128]{3,0,1,2:T(8,128)(2,1)S(1)}, bf16[192,8,4,128]{3,0,1,2:T(8,128)(2,1)}, u32[]{:S(2)}) copy-start(bf16[192,8,4,128]{3,0,1,2:T(8,128)(2,1)} %copy.24) | copy-start | bytes 4718596
  188.7 1.4 copy-start.4
  192.2 10.2 %all-to-all-start.3 = ((bf16[64,4,128]{2,1,0:T(4,128)(2,1)}), bf16[64,4,128]{2,1,0:T(4,128)(2,1)S(1)}, u32[]{:S(2)}, u32[]{:S(2)}) async-start(bf16[64,4,128]{2,1,0:T(4,128)(2,1)} %copy.27), calls=%async_computation.3 | async-start | bytes 131072 | tf_op jit(solution)/shard_map/all_to_all | solution.py:72
  334.5 1.2 copy-start.3
Sparse Core Ops, SparseCore 0:
  10.1 193.4 all-gather.6
  205.7 123.4 all-gather.4
